TPU v7x, 32 devices: a whole 2x2x4 slice. The times are simulated.
32 devices in a mesh: gx: 4 (over y, x), gy: 8 (over z, core).
Axes of the slice: x: 2, y: 2, z: 4, core: 2. Of those that a mesh axis runs over, the one named last changes fastest.
Arguments:
- fine_nodes: bfloat16 [65536, 256], P(('gx', 'gy')), may hold values from -6 to 6
- fine_weights: bfloat16 [6, 256, 256], replicated, may hold values from -0.375 to 0.375
- coarse_weights: bfloat16 [6, 256, 256], replicated, may hold values from -0.375 to 0.375
- top_weights: bfloat16 [6, 256, 256], replicated, may hold values from -0.375 to 0.375
- gains: float32 [3, 256], replicated, may hold values from 0.1 to 1.9
- send_list: int32 [4, 8, 4, 512], P('gx', 'gy'), may hold values from 0 to 2047
- fine_sender: int32 [4, 8, 8192], P('gx', 'gy'), may hold values from 0 to 4095, as said below
- fine_receiver: int32 [4, 8, 8192], P('gx', 'gy'), may hold values from 0 to 2048, as said below
- pool_owner: int32 [65536, 1], P(('gx', 'gy')), may hold values from 0 to 3; in each aligned block of 2048 rows (0 to 2047, 2048 to 4095, ...) at most 1024 rows name the same one
- pool_local: int32 [65536], P(('gx', 'gy')), may hold values from 0 to 255
- coarse_sender: int32 [8, 4096], P('gy', 'gx'), may hold values from 0 to 1023
- coarse_receiver: int32 [8, 4096], P('gy', 'gx'), may hold values from 0 to 255
- top_parent: int32 [8, 1024], P('gy', 'gx'), may hold values from 0 to 127
- top_sender: int32 [8, 512], P('gy'), may hold values from 0 to 127
- top_receiver: int32 [8, 512], P('gy'), may hold values from 0 to 127
Outputs:
- fine_state: bfloat16 [65536, 256], P(('gx', 'gy'))
- coarse_state: bfloat16 [8, 1024, 256], P('gy', 'gx')
Inputs may be any that keep to these rules, and one draw needn't show every extreme that they name: `fine_sender`: values below 2048 name the device's own nodes; larger values name a halo row of a neighbour that exists. `fine_receiver`: 2048 marks an empty slot; a device's live slots come first, and some device has no empty slot. `pool_owner`: among the rows of one device no member is named more than 1024 times.
All inputs are finite; a program needn't handle non-finite values.
Results may differ from a plain program's by a relative error of at most 0.015.
Values may be sent and summed in bfloat16 or wider, within the bound.
No kernel may reach another device: no remote copies, remote signals or barrier semaphores. Data moves between devices by JAX's collectives and lax.ppermute only.
A program may use at most 64 MiB of HBM per device.

v0:
```python
import math
import jax
import jax.numpy as jnp
from jax import lax
from jax.sharding import PartitionSpec as P


def passed_along(block, axis, distance):
    devices = range(lax.axis_size(axis))
    route = [(i - distance, i) for i in devices if i - distance in devices]
    return lax.ppermute(block, axis, route)


def project(states, weights):
    sender_term = jnp.dot(states, weights[0], preferred_element_type=jnp.float32).astype(
        jnp.bfloat16
    )
    receiver_term = jnp.dot(states, weights[1], preferred_element_type=jnp.float32).astype(
        jnp.bfloat16
    )
    return (sender_term, receiver_term)


def gather_messages(fetch, receiver_term, receivers, weight_out, count, most):
    edges = receivers.shape[0]
    block = math.gcd(edges, most)
    width = receiver_term.shape[1]

    def advance(summed, turn):
        begin = turn * block
        targets = lax.dynamic_slice_in_dim(receivers, begin, block)
        before = fetch(begin, block) + jnp.take(
            receiver_term, jnp.minimum(targets, count - 1), axis=0
        ).astype(jnp.float32)
        hidden = jax.nn.silu(before).astype(jnp.bfloat16)
        message = jnp.dot(hidden, weight_out, preferred_element_type=jnp.float32)
        return (summed.at[targets].add(message, mode="drop"), None)

    turns = jnp.arange(edges // block, dtype=jnp.int32)
    summed, unused = lax.scan(advance, jnp.zeros((count, width), jnp.float32), turns)
    return summed


def update_nodes(states, aggregate, weights, gain):
    merged = jnp.dot(states, weights[3], preferred_element_type=jnp.float32)
    merged = merged + jnp.dot(
        aggregate.astype(jnp.bfloat16), weights[4], preferred_element_type=jnp.float32
    )
    inner = jax.nn.silu(merged).astype(jnp.bfloat16)
    output = jnp.dot(inner, weights[5], preferred_element_type=jnp.float32)
    centred = output - jnp.mean(output, axis=1, keepdims=True)
    spread = jnp.mean(centred * centred, axis=1, keepdims=True)
    return (states.astype(jnp.float32) + gain * centred * lax.rsqrt(spread + 1e-05)).astype(
        jnp.bfloat16
    )


def table_fetch(table, senders):

    def fetch(begin, rows):
        picked = lax.dynamic_slice_in_dim(senders, begin, rows)
        return jnp.take(table, picked, axis=0).astype(jnp.float32)

    return fetch


def body(
    fine_nodes,
    fine_weights,
    coarse_weights,
    top_weights,
    gains,
    send_list,
    fine_sender,
    fine_receiver,
    pool_owner,
    pool_local,
    coarse_sender,
    coarse_receiver,
    top_parent,
    top_sender,
    top_receiver,
):
    nodes = fine_nodes.shape[0]
    width = fine_nodes.shape[1]
    members = lax.axis_size("gx")
    coarse_rows = nodes // 8
    top_rows = coarse_rows * members // 8
    lists = send_list.reshape(4, -1)
    fine_send, fine_recv = project(fine_nodes, fine_weights)
    pieces = [fine_send]
    for slot, offset in ((0, 1), (1, -1)):
        pieces.append(passed_along(jnp.take(fine_send, lists[slot], axis=0), "gx", offset))
    for slot, offset in ((2, 1), (3, -1)):
        pieces.append(passed_along(jnp.take(fine_send, lists[slot], axis=0), "gy", offset))
    table = jnp.concatenate(pieces, axis=0)
    fine_aggregate = gather_messages(
        table_fetch(table, fine_sender.reshape(-1)),
        fine_recv,
        fine_receiver.reshape(-1),
        fine_weights[2],
        nodes,
        4096,
    )
    fine_one = update_nodes(fine_nodes, fine_aggregate, fine_weights, gains[0])
    owner = pool_owner.reshape(-1)
    parent = owner * coarse_rows + pool_local
    partial_value = (
        jnp.zeros((members * coarse_rows, width), jnp.float32)
        .at[parent]
        .add(fine_one.astype(jnp.float32))
    )
    partial_count = jnp.zeros((members * coarse_rows,), jnp.float32).at[parent].add(1.0)
    coarse_sum, child_count = (
        lax.psum_scatter(
            partial_value.astype(jnp.bfloat16), "gx", scatter_dimension=0, tiled=True
        ).astype(jnp.float32),
        lax.psum_scatter(
            partial_count.astype(jnp.bfloat16), "gx", scatter_dimension=0, tiled=True
        ).astype(jnp.float32),
    )
    coarse_zero = (coarse_sum / jnp.maximum(child_count, 1.0)[:, None]).astype(jnp.bfloat16)
    coarse_send, coarse_recv = project(coarse_zero, coarse_weights)
    coarse_senders = coarse_sender.reshape(-1)
    piece = lax.all_gather(coarse_send, "gx", axis=0, tiled=True)
    inside = (coarse_senders >= 0) & (coarse_senders < piece.shape[0])
    picked = jnp.take(piece, jnp.clip(coarse_senders, 0, piece.shape[0] - 1), axis=0).astype(
        jnp.float32
    )
    gathered = jnp.where(inside[:, None], picked, 0.0)

    def slice_gathered(begin, rows):
        return gathered

    coarse_aggregate = gather_messages(
        slice_gathered,
        coarse_recv,
        coarse_receiver.reshape(-1),
        coarse_weights[2],
        coarse_rows,
        4096,
    )
    coarse_one = update_nodes(coarse_zero, coarse_aggregate, coarse_weights, gains[1])
    parents = top_parent.reshape(-1)
    partial_top = (
        jnp.zeros((top_rows, width), jnp.float32).at[parents].add(coarse_one.astype(jnp.float32))
    )
    partial_top_count = jnp.zeros((top_rows,), jnp.float32).at[parents].add(1.0)
    top_sum, top_count = (
        lax.psum(partial_top.astype(jnp.bfloat16), "gx").astype(jnp.float32),
        lax.psum(partial_top_count.astype(jnp.bfloat16), "gx").astype(jnp.float32),
    )
    top_zero = (top_sum / jnp.maximum(top_count, 1.0)[:, None]).astype(jnp.bfloat16)
    top_send, top_recv = project(top_zero, top_weights)
    top_aggregate = gather_messages(
        table_fetch(top_send, top_sender.reshape(-1)),
        top_recv,
        top_receiver.reshape(-1),
        top_weights[2],
        top_rows,
        4096,
    )
    top_one = update_nodes(top_zero, top_aggregate, top_weights, gains[2])
    coarse_two = (
        coarse_one.astype(jnp.float32) + jnp.take(top_one, parents, axis=0).astype(jnp.float32)
    ).astype(jnp.bfloat16)
    whole = lax.all_gather(coarse_two, "gx", axis=0, tiled=True)
    lifted = jnp.take(whole, parent, axis=0)
    fine_state = (fine_one.astype(jnp.float32) + lifted.astype(jnp.float32)).astype(jnp.bfloat16)
    return (fine_state, coarse_two[None])


def solution(mesh):
    placed = (
        P(("gx", "gy"), None),
        P(),
        P(),
        P(),
        P(),
        P("gx", "gy", None, None),
        P("gx", "gy", None),
        P("gx", "gy", None),
        P(("gx", "gy"), None),
        P(("gx", "gy")),
        P("gy", "gx"),
        P("gy", "gx"),
        P("gy", "gx"),
        P("gy", None),
        P("gy", None),
    )
    return jax.shard_map(
        body,
        mesh=mesh,
        in_specs=placed,
        out_specs=(P(("gx", "gy"), None), P("gy", "gx", None)),
        check_vma=False,
    )
```

profile of v0, /device:TPU:0, one launch (start us, length us, event | category | flops | bytes accessed | tf_op | source)
XLA Modules:
  0.0 395.7 jit_solution(5768898327504365994)
XLA Ops:
  12.6 5.6 %collective-permute-start = (bf16[512,256]{1,0:T(8,128)(2,1)}, bf16[512,256]{1,0:T(8,128)(2,1)}, u32[]{:S(2)}, u32[]{:S(2)}) collective-permute-start(bf16[512,256]{1,0:T(8,128)(2,1)} %broadcast_select_fusion.3), channel_id=1, source_target_pairs={{0,8},{8,16},{16,24},{1,9},{9,17},{17,25},{2,10},{10,18},{18,26},{... | collective-permute-start | bytes 786440 | tf_op jit(solution)/shard_map/ppermute | solution.py:11
  25.1 2.1 collective-permute-start.2
  34.7 2.7 fusion.46
  41.0 14.7 %scatter_custom_fusion.2 = f32[1024]{0:T(1024)S(1)} fusion(s32[2048]{0:T(1024)S(1)} %get-tuple-element.111, f32[2048]{0:T(1024)S(1)} %broadcast.313, f32[]{:T(128)} %constant.135.clone.1), kind=kCustom, calls=%fused_computation.167 | custom fusion | flops 2048 | bytes 4100 | tf_op jit(solution)/shard_map/scatter-add | solution.py:113
  55.7 2.3 scatter_custom_fusion.5
  59.2 11.6 %all-reduce.1 = (bf16[1024]{0:T(1024)(128)(2,1)}, bf16[128]{0:T(256)(128)(2,1)S(1)}) all-reduce(bf16[1024]{0:T(1024)(128)(2,1)S(1)} %convert_element_type.145, bf16[128]{0:T(256)(128)(2,1)S(1)} %convert_element_type.160), channel_id=3, replica_groups=mesh['gx'=4,'gy'=8] {'gx'}, use_global_device_ids=true, to_apply=%region_8.10.clone | all-reduce | flops 1152 | bytes 4608
  71.9 2.3 copy.34
  80.1 131.3 %while.2 = (s32[]{:T(128)}, f32[2048,256]{1,0:T(8,128)S(1)}, s32[2]{0:T(128)S(1)}, s32[8192]{0:T(1024)S(1)}, s32[8192]{0:T(1024)S(1)}, /*index=5*/bf16[4096,256]...) while((s32[]{:T(128)}, f32[2048,256]{1,0:T(8,128)S(1)}, ...), condition=%wide.region_2.4_spmd, body=%wide.region_0.3_spmd.sunk | while | flops 548507648 | bytes 30195924 | solution.py:40
  81.3 17.0 %gather_fusion = bf16[4096,256]{1,0:T(8,128)(2,1)} fusion(bf16[2048,256]{1,0:T(8,128)(2,1)S(1)} %get-tuple-element.235, s32[4096]{0:T(1024)S(1)} %get-tuple-element.201), kind=kCustom, calls=%fused_computation.2.clone.1 | custom fusion | bytes 4210688 | tf_op jit(solution)/shard_map/while/body/eval_jaxpr/jit(_take)/gather | solution.py:32
  98.3 17.7 %gather_fusion.1 = bf16[4096,256]{1,0:T(8,128)(2,1)} fusion(bf16[4096,256]{1,0:T(8,128)(2,1)} %get-tuple-element.234, s32[4096]{0:T(1024)S(1)} %get-tuple-element.202), kind=kCustom, calls=%fused_computation.1.clone.1 | custom fusion | bytes 4210688 | tf_op jit(solution)/shard_map/while/body/eval_jaxpr/jit(_take)/gather | solution.py:62
  116.0 6.1 %fusion.123 = f32[4096,256]{1,0:T(8,128)} fusion(bf16[256,256]{1,0:T(8,128)(2,1)S(1)} %copy-done.6, bf16[4096,256]{1,0:T(8,128)(2,1)} %gather_fusion, bf16[4096,256]{1,0:T(8,128)(2,1)} %gather_fusion.1, pred[4096]{0:T(1024)(128)(4,1)S(1)} %get-tuple-element.203, pred[4096]{0:T(1024)(128)(4,1)S(1)} %get-tuple-element.204), kind=kOutput, calls=%fused_computation.20.clone.1 | convolution fusion | flops 547356672 | bytes 8527872 | tf_op jit(solution)/shard_map/while/body/eval_jaxpr/dot_general | solution.py:36
  122.2 23.6 %scatter_fusion = f32[2048,256]{1,0:T(8,128)S(1)} fusion(f32[2048,256]{1,0:T(8,128)S(1)} %get-tuple-element.218, s32[4096]{0:T(1024)S(1)} %get-tuple-element.200, f32[4096,256]{1,0:T(8,128)} %fusion.123), kind=kCustom, calls=%fused_computation.12.clone.1 | custom fusion | flops 1048576 | bytes 12599296 | tf_op jit(solution)/shard_map/while/body/eval_jaxpr/scatter-add | solution.py:37
  147.0 17.0 %gather_fusion = bf16[4096,256]{1,0:T(8,128)(2,1)} fusion(bf16[2048,256]{1,0:T(8,128)(2,1)S(1)} %get-tuple-element.235, s32[4096]{0:T(1024)S(1)} %get-tuple-element.201), kind=kCustom, calls=%fused_computation.2.clone.1 | custom fusion | bytes 4210688 | tf_op jit(solution)/shard_map/while/body/eval_jaxpr/jit(_take)/gather | solution.py:32
  163.9 17.7 %gather_fusion.1 = bf16[4096,256]{1,0:T(8,128)(2,1)} fusion(bf16[4096,256]{1,0:T(8,128)(2,1)} %get-tuple-element.234, s32[4096]{0:T(1024)S(1)} %get-tuple-element.202), kind=kCustom, calls=%fused_computation.1.clone.1 | custom fusion | bytes 4210688 | tf_op jit(solution)/shard_map/while/body/eval_jaxpr/jit(_take)/gather | solution.py:62
  181.7 6.1 %fusion.123 = f32[4096,256]{1,0:T(8,128)} fusion(bf16[256,256]{1,0:T(8,128)(2,1)S(1)} %copy-done.6, bf16[4096,256]{1,0:T(8,128)(2,1)} %gather_fusion, bf16[4096,256]{1,0:T(8,128)(2,1)} %gather_fusion.1, pred[4096]{0:T(1024)(128)(4,1)S(1)} %get-tuple-element.203, pred[4096]{0:T(1024)(128)(4,1)S(1)} %get-tuple-element.204), kind=kOutput, calls=%fused_computation.20.clone.1 | convolution fusion | flops 547356672 | bytes 8527872 | tf_op jit(solution)/shard_map/while/body/eval_jaxpr/dot_general | solution.py:36
  187.8 23.6 %scatter_fusion = f32[2048,256]{1,0:T(8,128)S(1)} fusion(f32[2048,256]{1,0:T(8,128)S(1)} %get-tuple-element.218, s32[4096]{0:T(1024)S(1)} %get-tuple-element.200, f32[4096,256]{1,0:T(8,128)} %fusion.123), kind=kCustom, calls=%fused_computation.12.clone.1 | custom fusion | flops 1048576 | bytes 12599296 | tf_op jit(solution)/shard_map/while/body/eval_jaxpr/scatter-add | solution.py:37
  211.5 3.8 fusion.99
  221.1 13.0 %scatter_custom_fusion.1 = f32[1024,256]{1,0:T(8,128)} fusion(s32[2048]{0:T(1024)S(1)} %copy-done.11, f32[2048,256]{1,0:T(8,128)} %copy.35, f32[]{:T(128)} %constant.135.clone.1), kind=kCustom, calls=%fused_computation.52 | custom fusion | flops 524288 | bytes 1049088 | tf_op jit(solution)/shard_map/scatter-add | solution.py:111
  234.1 2.2 copy.36
  237.2 26.1 %reduce-scatter.2.cloned.1.call-done = bf16[256,256]{0,1:T(8,128)(2,1)} async-done(((bf16[1024,256]{0,1:T(8,128)(2,1)}), bf16[256,256]{0,1:T(8,128)(2,1)}) %reduce-scatter.2.cloned.1.call-update) | async-done | bytes 131088 | tf_op jit(solution)/shard_map/reduce_scatter | solution.py:115
  264.6 10.5 %all_gather.6 = bf16[1024,256]{1,0:T(8,128)(2,1)S(1)} all-gather(bf16[256,256]{1,0:T(8,128)(2,1)S(1)} %convolution_convert_fusion.3), channel_id=1, replica_groups=mesh['gx'=4,'gy'=8] {'gx'}, dimensions={0}, use_global_device_ids=true | all-gather | bytes 655360 | tf_op jit(solution)/shard_map/all_gather | solution.py:125
  275.1 3.9 gather_fusion.2
  280.2 5.0 %gather_fusion.3 = bf16[1024,256]{1,0:T(8,128)(2,1)} fusion(bf16[256,256]{1,0:T(8,128)(2,1)S(1)} %convolution_convert_fusion.2, s32[1024]{0:T(1024)S(1)} %get-tuple-element.140), kind=kCustom, calls=%fused_computation.9 | custom fusion | bytes 1052672 | tf_op jit(solution)/shard_map/while/body/eval_jaxpr/jit(_take)/gather | solution.py:32
  285.1 2.7 fusion.15
  287.8 6.6 %scatter_custom_fusion.3 = f32[256,256]{1,0:T(8,128)S(1)} fusion(s32[1024]{0:T(1024)S(1)} %bitcast.137, f32[1024,256]{1,0:T(8,128)} %fusion.15, f32[]{:T(128)} %constant.135.clone.1), kind=kCustom, calls=%fused_computation.112 | custom fusion | flops 262144 | bytes 262656 | tf_op jit(solution)/shard_map/while/body/eval_jaxpr/scatter-add | solution.py:37
  300.8 42.0 %all-reduce.4.cloned.1.call-done = bf16[128,256]{1,0:T(8,128)(2,1)} async-done(((bf16[128,256]{1,0:T(8,128)(2,1)}), bf16[128,256]{1,0:T(8,128)(2,1)}) %all-reduce.4.cloned.1.call-update) | async-done | bytes 65552 | tf_op jit(solution)/shard_map/psum | solution.py:150
  351.1 4.1 %scatter_custom_fusion.6 = f32[128,256]{1,0:T(8,128)S(1)} fusion(s32[512]{0:T(512)} %bitcast.142, f32[512,256]{1,0:T(8,128)} %fusion.21, f32[]{:T(128)} %constant.135.clone.1), kind=kCustom, calls=%fused_computation.123 | custom fusion | flops 131072 | bytes 131584 | tf_op jit(solution)/shard_map/while/body/eval_jaxpr/scatter-add | solution.py:37
  359.4 12.5 %all_gather.7 = bf16[1024,256]{0,1:T(8,128)(2,1)S(1)} all-gather(bf16[256,256]{0,1:T(8,128)(2,1)S(1)} %add_convert_fusion.2), channel_id=1, replica_groups=mesh['gx'=4,'gy'=8] {'gx'}, dimensions={0}, use_global_device_ids=true | all-gather | bytes 655360 | tf_op jit(solution)/shard_map/all_gather | solution.py:167
  372.0 9.1 %gather_fusion.5 = bf16[2048,256]{1,0:T(8,128)(2,1)} fusion(bf16[1024,256]{1,0:T(8,128)(2,1)S(1)} %copy.39, s32[2048]{0:T(1024)S(1)} %broadcast_clamp_fusion), kind=kCustom, calls=%fused_computation.11 | custom fusion | bytes 2105344 | tf_op jit(solution)/shard_map/jit(_take)/gather | solution.py:168
  381.1 2.3 copy.40
  383.4 2.5 add_convert_fusion
  385.9 2.3 copy.41
  (177 shorter events, 60.5 us)
Async XLA Ops:
  7.2 256.2 %reduce-scatter.2.cloned.1.call-start = ((), (), s32[]{:S(2)}) async-start(), calls=%async_computation.1 | async-start | bytes 655360 | tf_op jit(solution)/shard_map/reduce_scatter | solution.py:115
  12.6 63.0 %collective-permute-start = (bf16[512,256]{1,0:T(8,128)(2,1)}, bf16[512,256]{1,0:T(8,128)(2,1)}, u32[]{:S(2)}, u32[]{:S(2)}) collective-permute-start(bf16[512,256]{1,0:T(8,128)(2,1)} %broadcast_select_fusion.3), channel_id=1, source_target_pairs={{0,8},{8,16},{16,24},{1,9},{9,17},{17,25},{2,10},{10,18},{18,26},{... | collective-permute-start | bytes 786440 | tf_op jit(solution)/shard_map/ppermute | solution.py:11
  21.0 55.6 %collective-permute-start.1 = (bf16[512,256]{1,0:T(8,128)(2,1)}, bf16[512,256]{1,0:T(8,128)(2,1)}, u32[]{:S(2)}, u32[]{:S(2)}) collective-permute-start(bf16[512,256]{1,0:T(8,128)(2,1)} %broadcast_select_fusion.2), channel_id=1, source_target_pairs={{8,0},{16,8},{24,16},{9,1},{17,9},{25,17},{10,2},{18,10},{26,18},{... | collective-permute-start | bytes 786440 | tf_op jit(solution)/shard_map/ppermute | solution.py:11
  25.1 52.5 %collective-permute-start.2 = (bf16[512,256]{1,0:T(8,128)(2,1)}, bf16[512,256]{1,0:T(8,128)(2,1)}, u32[]{:S(2)}, u32[]{:S(2)}) collective-permute-start(bf16[512,256]{1,0:T(8,128)(2,1)} %broadcast_select_fusion.1), channel_id=1, source_target_pairs={{0,1},{1,2},{2,3},{3,4},{4,5},{5,6},{6,7},{8,9},{9,10},{10,11},{11... | collective-permute-start | bytes 786440 | tf_op jit(solution)/shard_map/ppermute | solution.py:11
  29.2 5.5 %copy-start.1 = (bf16[2048,256]{1,0:T(8,128)(2,1)S(1)}, bf16[2048,256]{1,0:T(8,128)(2,1)}, u32[]{:S(2)}) copy-start(bf16[2048,256]{1,0:T(8,128)(2,1)} %param.21) | copy-start | bytes 3145732
  30.1 48.5 %collective-permute-start.3 = (bf16[512,256]{1,0:T(8,128)(2,1)}, bf16[512,256]{1,0:T(8,128)(2,1)S(1)}, u32[]{:S(2)}, u32[]{:S(2)}) collective-permute-start(bf16[512,256]{1,0:T(8,128)(2,1)} %broadcast_select_fusion), channel_id=1, source_target_pairs={{1,0},{2,1},{3,2},{4,3},{5,4},{6,5},{7,6},{9,8},{10,9},{11,10},{12... | collective-permute-start | bytes 786440 | tf_op jit(solution)/shard_map/ppermute | solution.py:11
  33.0 5.6 %copy-start.23 = (s32[1,512]{1,0:T(1,128)S(1)}, s32[1,512]{1,0:T(1,128)}, u32[]{:S(2)}) copy-start(s32[1,512]{1,0:T(1,128)} %param.35) | copy-start | bytes 6148
  33.1 5.6 %copy-start.22 = (s32[1,512]{1,0:T(1,128)S(1)}, s32[1,512]{1,0:T(1,128)}, u32[]{:S(2)}) copy-start(s32[1,512]{1,0:T(1,128)} %param.34) | copy-start | bytes 6148
  33.1 6.7 %copy-start.29 = (f32[3,256]{1,0:T(4,128)S(1)}, f32[3,256]{1,0:T(4,128)}, u32[]{:S(2)}) copy-start(f32[3,256]{1,0:T(4,128)} %param.25) | copy-start | bytes 9220
  33.1 7.3 %copy-start.20 = (s32[2048,1]{0,1:T(1,128)S(1)}, s32[2048,1]{0,1:T(1,128)}, u32[]{:S(2)}) copy-start(s32[2048,1]{0,1:T(1,128)} %param.29) | copy-start | bytes 24580
  33.1 7.3 %copy-start.21 = (s32[2048]{0:T(1024)S(1)}, s32[2048]{0:T(1024)}, u32[]{:S(2)}) copy-start(s32[2048]{0:T(1024)} %param.30) | copy-start | bytes 24580
  33.1 22.6 %copy-start.30 = (s32[1,256]{1,0:T(1,128)S(1)}, s32[1,256]{1,0:T(1,128)}, u32[]{:S(2)}) copy-start(s32[1,256]{1,0:T(1,128)} %param.33) | copy-start | bytes 3076
  33.1 24.9 %copy-start.12 = (s32[1,1024]{1,0:T(1,128)S(1)}, s32[1,1024]{1,0:T(1,128)}, u32[]{:S(2)}) copy-start(s32[1,1024]{1,0:T(1,128)} %param.32) | copy-start | bytes 12292
  34.7 39.5 %copy-start.35 = (u32[32]{0:T(128)S(1)}, u32[32]{0:T(128)}, u32[]{:S(2)}) copy-start(u32[32]{0:T(128)} %constant.209) | copy-start | bytes 388
  41.0 37.6 %copy-start.10 = (s32[2048]{0:T(1024)}, s32[2048]{0:T(1024)S(1)}, u32[]{:S(2)}) copy-start(s32[2048]{0:T(1024)S(1)} %get-tuple-element.111) | copy-start | bytes 24580
  55.7 22.9 %copy-start.26 = (s32[256,1]{0,1:T(1,128)}, s32[256,1]{0,1:T(1,128)S(1)}, u32[]{:S(2)}) copy-start(s32[256,1]{0,1:T(1,128)S(1)} %compare_select_fusion.10) | copy-start | bytes 3076
  75.6 4.5 %copy-start.3 = (s32[1,1,8192]{2,1,0:T(1,128)S(1)}, s32[1,1,8192]{2,1,0:T(1,128)}, u32[]{:S(2)}) copy-start(s32[1,1,8192]{2,1,0:T(1,128)} %param.28) | copy-start | bytes 98308
  75.6 4.5 %copy-start.4 = (s32[1,1,8192]{2,1,0:T(1,128)S(1)}, s32[1,1,8192]{2,1,0:T(1,128)}, u32[]{:S(2)}) copy-start(s32[1,1,8192]{2,1,0:T(1,128)} %param.27) | copy-start | bytes 98308
  98.3 17.8 %copy-start.6 = (bf16[256,256]{1,0:T(8,128)(2,1)S(1)}, bf16[256,256]{1,0:T(8,128)(2,1)}, u32[]{:S(2)}) copy-start(bf16[256,256]{1,0:T(8,128)(2,1)} %get-tuple-element.236) | copy-start | bytes 393220 | tf_op jit(solution)/shard_map/while
  163.9 17.8 %copy-start.6 = (bf16[256,256]{1,0:T(8,128)(2,1)S(1)}, bf16[256,256]{1,0:T(8,128)(2,1)}, u32[]{:S(2)}) copy-start(bf16[256,256]{1,0:T(8,128)(2,1)} %get-tuple-element.236) | copy-start | bytes 393220 | tf_op jit(solution)/shard_map/while
  221.1 16.0 %copy-start.9 = (s32[1,1024]{1,0:T(1,128)S(1)}, s32[1,1024]{1,0:T(1,128)}, u32[]{:S(2)}) copy-start(s32[1,1024]{1,0:T(1,128)} %param.31) | copy-start | bytes 12292
  221.1 16.0 %copy-start.14 = (s32[1,1024]{1,0:T(1,128)S(1)}, s32[1,1024]{1,0:T(1,128)}, u32[]{:S(2)}) copy-start(s32[1,1024]{1,0:T(1,128)} %broadcast_clamp_fusion.3) | copy-start | bytes 12292
  221.1 16.0 %copy-start.15 = (s32[1,1024]{1,0:T(1,128)S(1)}, s32[1,1024]{1,0:T(1,128)}, u32[]{:S(2)}) copy-start(s32[1,1024]{1,0:T(1,128)} %broadcast_minimum_fusion) | copy-start | bytes 12292
  221.1 16.1 %copy-start.13 = (s32[1,1024]{1,0:T(1,128)S(1)}, s32[1,1024]{1,0:T(1,128)}, u32[]{:S(2)}) copy-start(s32[1,1024]{1,0:T(1,128)} %param.32) | copy-start | bytes 12292
  221.1 16.1 %copy-start.16 = (s32[1024,1]{0,1:T(1,128)S(1)}, s32[1024,1]{0,1:T(1,128)}, u32[]{:S(2)}) copy-start(s32[1024,1]{0,1:T(1,128)} %compare_select_fusion.4) | copy-start | bytes 12292
  236.3 106.4 %all-reduce.4.cloned.1.call-start = ((), (), s32[]{:S(2)}) async-start(), calls=%async_computation.2 | async-start | bytes 131072 | tf_op jit(solution)/shard_map/psum | solution.py:150
  287.8 10.0 %copy-start.25 = (f32[1,256]{1,0:T(1,128)S(1)}, f32[1,256]{1,0:T(1,128)}, u32[]{:S(2)}) copy-start(f32[1,256]{1,0:T(1,128)} %get-tuple-element.123) | copy-start | bytes 3076
  294.4 48.3 %copy-start.32 = (f32[128]{0:T(128)S(1)}, f32[128]{0:T(128)}, u32[]{:S(2)}) copy-start(f32[128]{0:T(128)} %convert_maximum_fusion.1) | copy-start | bytes 1540
  296.3 47.6 %copy-start.18 = (s32[1024]{0:T(1024)S(1)}, s32[1024]{0:T(1024)}, u32[]{:S(2)}) copy-start(s32[1024]{0:T(1024)} %get-tuple-element.135) | copy-start | bytes 12292
  298.1 48.9 %copy-start.17 = (s32[1024]{0:T(1024)S(1)}, s32[1024]{0:T(1024)}, u32[]{:S(2)}) copy-start(s32[1024]{0:T(1024)} %get-tuple-element.134) | copy-start | bytes 12292
  349.0 8.9 %copy-start.24 = (f32[1,256]{1,0:T(1,128)S(1)}, f32[1,256]{1,0:T(1,128)}, u32[]{:S(2)}) copy-start(f32[1,256]{1,0:T(1,128)} %get-tuple-element.121) | copy-start | bytes 3076
  351.1 8.2 %copy-start.31 = (pred[256]{0:T(512)(128)(4,1)S(1)}, pred[256]{0:T(512)(128)(4,1)}, u32[]{:S(2)}) copy-start(pred[256]{0:T(512)(128)(4,1)} %compare_and_fusion.11) | copy-start | bytes 772
  (11 other events, 31.3 us)
Sparse Core Ops, SparseCore 0:
  236.4 26.8 reduce-scatter.1
  300.9 41.8 all-reduce.3
where the time goes:
time: 397 us; the launch traced here: 396 us
  local copies, waits for them, and re-layouts  122 us (31%)
  other arithmetic  107 us (27%)
  waiting for transfers between devices  68.2 us (17%)
  matrix products  37.3 us (9%)
  blocking collectives  34.5 us (9%)
  between operations  15.5 us (4%)
  starting transfers between devices  10.4 us (3%)
    scatter-add x4, other arithmetic, advance(): return (summed.at[targets].add(message, mode='drop'), None)  57.9 us
    psum x1, waiting for transfers between devices, body(): lax.psum(partial_top.astype(jnp.bfloat16), 'gx').astype(jnp.float32)  42 us
    gather x4, local copies, waits for them, and re-layouts, advance(): jnp.take(receiver_term, jnp.minimum(targets, count - 1), axis=0)  40.8 us
    gather x3, local copies, waits for them, and re-layouts, fetch(): return jnp.take(table, picked, axis=0).astype(jnp.float32)  37.4 us
    reduce_scatter x1, waiting for transfers between devices, body(): lax.psum_scatter(partial_value.astype(jnp.bfloat16), 'gx', scatter_dimens...  26.1 us
    dot_general x4, matrix products, advance(): message = jnp.dot(hidden, weight_out, preferred_element_type=jnp.float32)  17 us
    scatter-add x1, other arithmetic, body(): jnp.zeros((members * coarse_rows,), jnp.float32).at[parent].add(1.0)  14.7 us
    scatter-add x1, other arithmetic, body(): partial_value = jnp.zeros((members * coarse_rows, width), jnp.float32).at...  13 us
  transfers between devices with their start and end apart: 6, of which 2 were waited for; matrix products, arithmetic and copies ran while one was open for 11% of the time, Pallas kernels for 0%

commit v1 on v0

--- a/solution.py
+++ b/solution.py
@@ -147,7 +147,7 @@
     )
     partial_top_count = jnp.zeros((top_rows,), jnp.float32).at[parents].add(1.0)
     top_sum, top_count = (
-        lax.psum(partial_top.astype(jnp.bfloat16), "gx").astype(jnp.float32),
+        jnp.sum(lax.all_gather(partial_top.astype(jnp.bfloat16), "gx"), axis=0).astype(jnp.float32),
         lax.psum(partial_top_count.astype(jnp.bfloat16), "gx").astype(jnp.float32),
     )
     top_zero = (top_sum / jnp.maximum(top_count, 1.0)[:, None]).astype(jnp.bfloat16)

time: 397 us -> 363 us (0.914)
  waiting for transfers between devices: 68.2 us -> 26.2 us
  blocking collectives: 34.5 us -> 42.2 us
    psum x1 -> x0, waiting for transfers between devices: 42 us -> none  [body(): lax.psum(partial_top.astype(jnp.bfloat16), 'gx').astype(jnp.float32)]
    all_gather x0 -> x1, blocking collectives: none -> 7.77 us  [body(): lax.all_gather(partial_top.astype(jnp.bfloat16), 'gx')]
    unnamed x77 -> x73, local copies, waits for them, and re-layouts: 10.6 us -> 10.6 us
  transfers between devices with their start and end apart: 6 -> 5, of which waited for: 2 -> 1; matrix products, arithmetic and copies ran while one was open for 11% -> 12% of each run, Pallas kernels for 0% -> 0%
where the time goes in v1:
time: 363 us; the launch traced here: 361 us
  local copies, waits for them, and re-layouts  123 us (34%)
  other arithmetic  107 us (29%)
  blocking collectives  42.2 us (12%)
  matrix products  36.4 us (10%)
  waiting for transfers between devices  26.2 us (7%)
  between operations  15.5 us (4%)
  starting transfers between devices  10.3 us (3%)
    scatter-add x4, other arithmetic, advance(): return (summed.at[targets].add(message, mode='drop'), None)  57.9 us
    gather x4, local copies, waits for them, and re-layouts, advance(): jnp.take(receiver_term, jnp.minimum(targets, count - 1), axis=0)  40.9 us
    gather x3, local copies, waits for them, and re-layouts, fetch(): return jnp.take(table, picked, axis=0).astype(jnp.float32)  37.6 us
    reduce_scatter x1, waiting for transfers between devices, body(): lax.psum_scatter(partial_value.astype(jnp.bfloat16), 'gx', scatter_dimens...  26.2 us
    dot_general x4, matrix products, advance(): message = jnp.dot(hidden, weight_out, preferred_element_type=jnp.float32)  17 us
    scatter-add x1, other arithmetic, body(): jnp.zeros((members * coarse_rows,), jnp.float32).at[parent].add(1.0)  14.7 us
    scatter-add x1, other arithmetic, body(): partial_value = jnp.zeros((members * coarse_rows, width), jnp.float32).at...  13 us
    all_gather x1, blocking collectives, body(): whole = lax.all_gather(coarse_two, 'gx', axis=0, tiled=True)  12.4 us
  transfers between devices with their start and end apart: 5, of which 1 were waited for; matrix products, arithmetic and copies ran while one was open for 12% of the time, Pallas kernels for 0%

profile of v1, /device:TPU:0, one launch (start us, length us, event | category | flops | bytes accessed | tf_op | source)
XLA Modules:
  0.0 361.5 jit_solution(15277060333593748989)
XLA Ops:
  12.6 5.6 %collective-permute-start = (bf16[512,256]{1,0:T(8,128)(2,1)}, bf16[512,256]{1,0:T(8,128)(2,1)}, u32[]{:S(2)}, u32[]{:S(2)}) collective-permute-start(bf16[512,256]{1,0:T(8,128)(2,1)} %broadcast_select_fusion.3), channel_id=1, source_target_pairs={{0,8},{8,16},{16,24},{1,9},{9,17},{17,25},{2,10},{10,18},{18,26},{... | collective-permute-start | bytes 786440 | tf_op jit(solution)/shard_map/ppermute | solution.py:11
  25.1 2.2 collective-permute-start.2
  34.7 2.7 fusion.46
  41.0 14.7 %scatter_custom_fusion.2 = f32[1024]{0:T(1024)S(1)} fusion(s32[2048]{0:T(1024)S(1)} %get-tuple-element.111, f32[2048]{0:T(1024)S(1)} %broadcast.313, f32[]{:T(128)} %constant.136.clone.1), kind=kCustom, calls=%fused_computation.167 | custom fusion | flops 2048 | bytes 4100 | tf_op jit(solution)/shard_map/scatter-add | solution.py:113
  55.8 2.3 scatter_custom_fusion.5
  59.2 11.6 %all-reduce.1 = (bf16[1024]{0:T(1024)(128)(2,1)}, bf16[128]{0:T(256)(128)(2,1)S(1)}) all-reduce(bf16[1024]{0:T(1024)(128)(2,1)S(1)} %convert_element_type.147, bf16[128]{0:T(256)(128)(2,1)S(1)} %convert_element_type.162), channel_id=4, replica_groups=mesh['gx'=4,'gy'=8] {'gx'}, use_global_device_ids=true, to_apply=%region_8.10.clone | all-reduce | flops 1152 | bytes 4608
  72.6 2.3 copy.34
  80.7 132.0 %while.2 = (s32[]{:T(128)}, f32[2048,256]{1,0:T(8,128)S(1)}, s32[2]{0:T(128)S(1)}, s32[8192]{0:T(1024)S(1)}, s32[8192]{0:T(1024)S(1)}, /*index=5*/bf16[4096,256]...) while((s32[]{:T(128)}, f32[2048,256]{1,0:T(8,128)S(1)}, ...), condition=%wide.region_2.4_spmd, body=%wide.region_0.3_spmd.sunk | while | flops 548507648 | bytes 30195924 | solution.py:40
  82.0 17.0 %gather_fusion = bf16[4096,256]{1,0:T(8,128)(2,1)} fusion(bf16[2048,256]{1,0:T(8,128)(2,1)S(1)} %get-tuple-element.235, s32[4096]{0:T(1024)S(1)} %get-tuple-element.201), kind=kCustom, calls=%fused_computation.2.clone.1 | custom fusion | bytes 4210688 | tf_op jit(solution)/shard_map/while/body/eval_jaxpr/jit(_take)/gather | solution.py:32
  99.0 17.8 %gather_fusion.1 = bf16[4096,256]{1,0:T(8,128)(2,1)} fusion(bf16[4096,256]{1,0:T(8,128)(2,1)} %get-tuple-element.234, s32[4096]{0:T(1024)S(1)} %get-tuple-element.202), kind=kCustom, calls=%fused_computation.1.clone.1 | custom fusion | bytes 4210688 | tf_op jit(solution)/shard_map/while/body/eval_jaxpr/jit(_take)/gather | solution.py:62
  116.9 6.1 %fusion.123 = f32[4096,256]{1,0:T(8,128)} fusion(bf16[256,256]{1,0:T(8,128)(2,1)S(1)} %copy-done.6, bf16[4096,256]{1,0:T(8,128)(2,1)} %gather_fusion, bf16[4096,256]{1,0:T(8,128)(2,1)} %gather_fusion.1, pred[4096]{0:T(1024)(128)(4,1)S(1)} %get-tuple-element.203, pred[4096]{0:T(1024)(128)(4,1)S(1)} %get-tuple-element.204), kind=kOutput, calls=%fused_computation.20.clone.1 | convolution fusion | flops 547356672 | bytes 8527872 | tf_op jit(solution)/shard_map/while/body/eval_jaxpr/dot_general | solution.py:36
  123.0 23.6 %scatter_fusion = f32[2048,256]{1,0:T(8,128)S(1)} fusion(f32[2048,256]{1,0:T(8,128)S(1)} %get-tuple-element.218, s32[4096]{0:T(1024)S(1)} %get-tuple-element.200, f32[4096,256]{1,0:T(8,128)} %fusion.123), kind=kCustom, calls=%fused_computation.12.clone.1 | custom fusion | flops 1048576 | bytes 12599296 | tf_op jit(solution)/shard_map/while/body/eval_jaxpr/scatter-add | solution.py:37
  148.0 17.0 %gather_fusion = bf16[4096,256]{1,0:T(8,128)(2,1)} fusion(bf16[2048,256]{1,0:T(8,128)(2,1)S(1)} %get-tuple-element.235, s32[4096]{0:T(1024)S(1)} %get-tuple-element.201), kind=kCustom, calls=%fused_computation.2.clone.1 | custom fusion | bytes 4210688 | tf_op jit(solution)/shard_map/while/body/eval_jaxpr/jit(_take)/gather | solution.py:32
  165.0 17.8 %gather_fusion.1 = bf16[4096,256]{1,0:T(8,128)(2,1)} fusion(bf16[4096,256]{1,0:T(8,128)(2,1)} %get-tuple-element.234, s32[4096]{0:T(1024)S(1)} %get-tuple-element.202), kind=kCustom, calls=%fused_computation.1.clone.1 | custom fusion | bytes 4210688 | tf_op jit(solution)/shard_map/while/body/eval_jaxpr/jit(_take)/gather | solution.py:62
  182.9 6.1 %fusion.123 = f32[4096,256]{1,0:T(8,128)} fusion(bf16[256,256]{1,0:T(8,128)(2,1)S(1)} %copy-done.6, bf16[4096,256]{1,0:T(8,128)(2,1)} %gather_fusion, bf16[4096,256]{1,0:T(8,128)(2,1)} %gather_fusion.1, pred[4096]{0:T(1024)(128)(4,1)S(1)} %get-tuple-element.203, pred[4096]{0:T(1024)(128)(4,1)S(1)} %get-tuple-element.204), kind=kOutput, calls=%fused_computation.20.clone.1 | convolution fusion | flops 547356672 | bytes 8527872 | tf_op jit(solution)/shard_map/while/body/eval_jaxpr/dot_general | solution.py:36
  189.0 23.6 %scatter_fusion = f32[2048,256]{1,0:T(8,128)S(1)} fusion(f32[2048,256]{1,0:T(8,128)S(1)} %get-tuple-element.218, s32[4096]{0:T(1024)S(1)} %get-tuple-element.200, f32[4096,256]{1,0:T(8,128)} %fusion.123), kind=kCustom, calls=%fused_computation.12.clone.1 | custom fusion | flops 1048576 | bytes 12599296 | tf_op jit(solution)/shard_map/while/body/eval_jaxpr/scatter-add | solution.py:37
  212.6 3.8 %fusion.99 = (f32[2048]{0:T(1024)S(1)}, f32[2048,256]{0,1:T(8,128)}) fusion(bf16[6,256,256]{2,1,0:T(8,128)(2,1)} %param.22, f32[2048,256]{1,0:T(8,128)} %fusion.46, f32[2048,256]{1,0:T(8,128)S(1)} %get-tuple-element.85), kind=kOutput, calls=%fused_computation.195 | convolution fusion | flops 541063168 | bytes 6561792 | tf_op jit(solution)/shard_map/dot_general | solution.py:50
  222.3 13.0 %scatter_custom_fusion.1 = f32[1024,256]{1,0:T(8,128)} fusion(s32[2048]{0:T(1024)S(1)} %copy-done.10, f32[2048,256]{1,0:T(8,128)} %copy.35, f32[]{:T(128)} %constant.136.clone.1), kind=kCustom, calls=%fused_computation.52 | custom fusion | flops 524288 | bytes 1049088 | tf_op jit(solution)/shard_map/scatter-add | solution.py:111
  235.3 2.2 copy.36
  238.4 26.2 %reduce-scatter.2.cloned.1.call-done = bf16[256,256]{0,1:T(8,128)(2,1)} async-done(((bf16[1024,256]{0,1:T(8,128)(2,1)}), bf16[256,256]{0,1:T(8,128)(2,1)}) %reduce-scatter.2.cloned.1.call-update) | async-done | bytes 131088 | tf_op jit(solution)/shard_map/reduce_scatter | solution.py:115
  265.8 10.5 %all_gather.12 = bf16[1024,256]{1,0:T(8,128)(2,1)S(1)} all-gather(bf16[256,256]{1,0:T(8,128)(2,1)S(1)} %convolution_convert_fusion.3), channel_id=1, replica_groups=mesh['gx'=4,'gy'=8] {'gx'}, dimensions={0}, use_global_device_ids=true | all-gather | bytes 655360 | tf_op jit(solution)/shard_map/all_gather | solution.py:125
  276.3 3.9 %gather_fusion.2 = bf16[1024,256]{1,0:T(8,128)(2,1)S(1)} fusion(bf16[1024,256]{1,0:T(8,128)(2,1)S(1)} %all_gather.12, s32[1024]{0:T(1024)S(1)} %get-tuple-element.141), kind=kCustom, calls=%fused_computation.8 | custom fusion | bytes 1052672 | tf_op jit(solution)/shard_map/jit(_take)/gather | solution.py:127
  281.4 5.0 %gather_fusion.3 = bf16[1024,256]{1,0:T(8,128)(2,1)} fusion(bf16[256,256]{1,0:T(8,128)(2,1)S(1)} %convolution_convert_fusion.2, s32[1024]{0:T(1024)S(1)} %get-tuple-element.140), kind=kCustom, calls=%fused_computation.9 | custom fusion | bytes 1052672 | tf_op jit(solution)/shard_map/while/body/eval_jaxpr/jit(_take)/gather | solution.py:32
  286.4 2.7 fusion.15
  289.0 6.6 %scatter_custom_fusion.3 = f32[256,256]{1,0:T(8,128)S(1)} fusion(s32[1024]{0:T(1024)S(1)} %bitcast.139, f32[1024,256]{1,0:T(8,128)} %fusion.15, f32[]{:T(128)} %constant.136.clone.1), kind=kCustom, calls=%fused_computation.112 | custom fusion | flops 262144 | bytes 262656 | tf_op jit(solution)/shard_map/while/body/eval_jaxpr/scatter-add | solution.py:37
  300.7 7.8 %all-gather = bf16[512,256]{1,0:T(8,128)(2,1)S(1)} all-gather(bf16[128,256]{1,0:T(8,128)(2,1)S(1)} %convert_element_type.160), channel_id=2, replica_groups=mesh['gx'=4,'gy'=8] {'gx'}, dimensions={0}, use_global_device_ids=true | all-gather | bytes 327680 | tf_op jit(solution)/shard_map/all_gather | solution.py:150
  318.0 4.1 %scatter_custom_fusion.6 = f32[128,256]{1,0:T(8,128)S(1)} fusion(s32[512]{0:T(512)} %bitcast.144, f32[512,256]{1,0:T(8,128)} %fusion.21, f32[]{:T(128)} %constant.136.clone.1), kind=kCustom, calls=%fused_computation.123 | custom fusion | flops 131072 | bytes 131584 | tf_op jit(solution)/shard_map/while/body/eval_jaxpr/scatter-add | solution.py:37
  325.2 12.4 %all_gather.15 = bf16[1024,256]{0,1:T(8,128)(2,1)S(1)} all-gather(bf16[256,256]{0,1:T(8,128)(2,1)S(1)} %add_convert_fusion.2), channel_id=1, replica_groups=mesh['gx'=4,'gy'=8] {'gx'}, dimensions={0}, use_global_device_ids=true | all-gather | bytes 655360 | tf_op jit(solution)/shard_map/all_gather | solution.py:167
  337.8 9.1 %gather_fusion.5 = bf16[2048,256]{1,0:T(8,128)(2,1)} fusion(bf16[1024,256]{1,0:T(8,128)(2,1)S(1)} %copy.39, s32[2048]{0:T(1024)S(1)} %broadcast_clamp_fusion), kind=kCustom, calls=%fused_computation.11 | custom fusion | bytes 2105344 | tf_op jit(solution)/shard_map/jit(_take)/gather | solution.py:168
  346.8 2.3 copy.40
  349.1 2.5 add_convert_fusion
  351.6 2.3 copy.41
  (172 shorter events, 60.0 us)
Async XLA Ops:
  7.2 257.4 %reduce-scatter.2.cloned.1.call-start = ((), (), s32[]{:S(2)}) async-start(), calls=%async_computation.1 | async-start | bytes 655360 | tf_op jit(solution)/shard_map/reduce_scatter | solution.py:115
  12.6 63.5 %collective-permute-start = (bf16[512,256]{1,0:T(8,128)(2,1)}, bf16[512,256]{1,0:T(8,128)(2,1)}, u32[]{:S(2)}, u32[]{:S(2)}) collective-permute-start(bf16[512,256]{1,0:T(8,128)(2,1)} %broadcast_select_fusion.3), channel_id=1, source_target_pairs={{0,8},{8,16},{16,24},{1,9},{9,17},{17,25},{2,10},{10,18},{18,26},{... | collective-permute-start | bytes 786440 | tf_op jit(solution)/shard_map/ppermute | solution.py:11
  21.0 56.2 %collective-permute-start.1 = (bf16[512,256]{1,0:T(8,128)(2,1)}, bf16[512,256]{1,0:T(8,128)(2,1)}, u32[]{:S(2)}, u32[]{:S(2)}) collective-permute-start(bf16[512,256]{1,0:T(8,128)(2,1)} %broadcast_select_fusion.2), channel_id=1, source_target_pairs={{8,0},{16,8},{24,16},{9,1},{17,9},{25,17},{10,2},{18,10},{26,18},{... | collective-permute-start | bytes 786440 | tf_op jit(solution)/shard_map/ppermute | solution.py:11
  25.1 53.0 %collective-permute-start.2 = (bf16[512,256]{1,0:T(8,128)(2,1)}, bf16[512,256]{1,0:T(8,128)(2,1)}, u32[]{:S(2)}, u32[]{:S(2)}) collective-permute-start(bf16[512,256]{1,0:T(8,128)(2,1)} %broadcast_select_fusion.1), channel_id=1, source_target_pairs={{0,1},{1,2},{2,3},{3,4},{4,5},{5,6},{6,7},{8,9},{9,10},{10,11},{11... | collective-permute-start | bytes 786440 | tf_op jit(solution)/shard_map/ppermute | solution.py:11
  29.2 5.5 %copy-start.1 = (bf16[2048,256]{1,0:T(8,128)(2,1)S(1)}, bf16[2048,256]{1,0:T(8,128)(2,1)}, u32[]{:S(2)}) copy-start(bf16[2048,256]{1,0:T(8,128)(2,1)} %param.21) | copy-start | bytes 3145732
  30.1 49.0 %collective-permute-start.3 = (bf16[512,256]{1,0:T(8,128)(2,1)}, bf16[512,256]{1,0:T(8,128)(2,1)S(1)}, u32[]{:S(2)}, u32[]{:S(2)}) collective-permute-start(bf16[512,256]{1,0:T(8,128)(2,1)} %broadcast_select_fusion), channel_id=1, source_target_pairs={{1,0},{2,1},{3,2},{4,3},{5,4},{6,5},{7,6},{9,8},{10,9},{11,10},{12... | collective-permute-start | bytes 786440 | tf_op jit(solution)/shard_map/ppermute | solution.py:11
  33.0 4.4 %copy-start.7 = (s32[1,1024]{1,0:T(1,128)S(1)}, s32[1,1024]{1,0:T(1,128)}, u32[]{:S(2)}) copy-start(s32[1,1024]{1,0:T(1,128)} %param.31) | copy-start | bytes 12292
  33.0 5.5 %copy-start.22 = (s32[1,512]{1,0:T(1,128)S(1)}, s32[1,512]{1,0:T(1,128)}, u32[]{:S(2)}) copy-start(s32[1,512]{1,0:T(1,128)} %param.35) | copy-start | bytes 6148
  33.1 5.6 %copy-start.21 = (s32[1,512]{1,0:T(1,128)S(1)}, s32[1,512]{1,0:T(1,128)}, u32[]{:S(2)}) copy-start(s32[1,512]{1,0:T(1,128)} %param.34) | copy-start | bytes 6148
  33.1 6.7 %copy-start.27 = (f32[3,256]{1,0:T(4,128)S(1)}, f32[3,256]{1,0:T(4,128)}, u32[]{:S(2)}) copy-start(f32[3,256]{1,0:T(4,128)} %param.25) | copy-start | bytes 9220
  33.1 7.3 %copy-start.19 = (s32[2048,1]{0,1:T(1,128)S(1)}, s32[2048,1]{0,1:T(1,128)}, u32[]{:S(2)}) copy-start(s32[2048,1]{0,1:T(1,128)} %param.29) | copy-start | bytes 24580
  33.1 7.3 %copy-start.20 = (s32[2048]{0:T(1024)S(1)}, s32[2048]{0:T(1024)}, u32[]{:S(2)}) copy-start(s32[2048]{0:T(1024)} %param.30) | copy-start | bytes 24580
  33.1 22.6 %copy-start.28 = (s32[1,256]{1,0:T(1,128)S(1)}, s32[1,256]{1,0:T(1,128)}, u32[]{:S(2)}) copy-start(s32[1,256]{1,0:T(1,128)} %param.33) | copy-start | bytes 3076
  33.1 25.0 %copy-start.11 = (s32[1,1024]{1,0:T(1,128)S(1)}, s32[1,1024]{1,0:T(1,128)}, u32[]{:S(2)}) copy-start(s32[1,1024]{1,0:T(1,128)} %param.32) | copy-start | bytes 12292
  34.7 40.1 %copy-start.33 = (u32[32]{0:T(128)S(1)}, u32[32]{0:T(128)}, u32[]{:S(2)}) copy-start(u32[32]{0:T(128)} %constant.211) | copy-start | bytes 388
  41.0 38.1 %copy-start.9 = (s32[2048]{0:T(1024)}, s32[2048]{0:T(1024)S(1)}, u32[]{:S(2)}) copy-start(s32[2048]{0:T(1024)S(1)} %get-tuple-element.111) | copy-start | bytes 24580
  55.7 23.4 %copy-start.25 = (s32[256,1]{0,1:T(1,128)}, s32[256,1]{0,1:T(1,128)S(1)}, u32[]{:S(2)}) copy-start(s32[256,1]{0,1:T(1,128)S(1)} %compare_select_fusion.10) | copy-start | bytes 3076
  76.1 4.5 %copy-start.3 = (s32[1,1,8192]{2,1,0:T(1,128)S(1)}, s32[1,1,8192]{2,1,0:T(1,128)}, u32[]{:S(2)}) copy-start(s32[1,1,8192]{2,1,0:T(1,128)} %param.28) | copy-start | bytes 98308
  76.1 4.5 %copy-start.4 = (s32[1,1,8192]{2,1,0:T(1,128)S(1)}, s32[1,1,8192]{2,1,0:T(1,128)}, u32[]{:S(2)}) copy-start(s32[1,1,8192]{2,1,0:T(1,128)} %param.27) | copy-start | bytes 98308
  99.0 17.9 %copy-start.6 = (bf16[256,256]{1,0:T(8,128)(2,1)S(1)}, bf16[256,256]{1,0:T(8,128)(2,1)}, u32[]{:S(2)}) copy-start(bf16[256,256]{1,0:T(8,128)(2,1)} %get-tuple-element.236) | copy-start | bytes 393220 | tf_op jit(solution)/shard_map/while
  165.0 17.9 %copy-start.6 = (bf16[256,256]{1,0:T(8,128)(2,1)S(1)}, bf16[256,256]{1,0:T(8,128)(2,1)}, u32[]{:S(2)}) copy-start(bf16[256,256]{1,0:T(8,128)(2,1)} %get-tuple-element.236) | copy-start | bytes 393220 | tf_op jit(solution)/shard_map/while
  222.3 16.0 %copy-start.8 = (s32[1,1024]{1,0:T(1,128)S(1)}, s32[1,1024]{1,0:T(1,128)}, u32[]{:S(2)}) copy-start(s32[1,1024]{1,0:T(1,128)} %param.31) | copy-start | bytes 12292
  222.3 16.0 %copy-start.13 = (s32[1,1024]{1,0:T(1,128)S(1)}, s32[1,1024]{1,0:T(1,128)}, u32[]{:S(2)}) copy-start(s32[1,1024]{1,0:T(1,128)} %broadcast_clamp_fusion.3) | copy-start | bytes 12292
  222.3 16.0 %copy-start.14 = (s32[1,1024]{1,0:T(1,128)S(1)}, s32[1,1024]{1,0:T(1,128)}, u32[]{:S(2)}) copy-start(s32[1,1024]{1,0:T(1,128)} %broadcast_minimum_fusion) | copy-start | bytes 12292
  222.3 16.1 %copy-start.12 = (s32[1,1024]{1,0:T(1,128)S(1)}, s32[1,1024]{1,0:T(1,128)}, u32[]{:S(2)}) copy-start(s32[1,1024]{1,0:T(1,128)} %param.32) | copy-start | bytes 12292
  222.3 16.1 %copy-start.15 = (s32[1024,1]{0,1:T(1,128)S(1)}, s32[1024,1]{0,1:T(1,128)}, u32[]{:S(2)}) copy-start(s32[1024,1]{0,1:T(1,128)} %compare_select_fusion.4) | copy-start | bytes 12292
  289.0 9.2 %copy-start.24 = (f32[1,256]{1,0:T(1,128)S(1)}, f32[1,256]{1,0:T(1,128)}, u32[]{:S(2)}) copy-start(f32[1,256]{1,0:T(1,128)} %get-tuple-element.123) | copy-start | bytes 3076
  296.8 11.7 %copy-start.30 = (f32[128]{0:T(128)S(1)}, f32[128]{0:T(128)}, u32[]{:S(2)}) copy-start(f32[128]{0:T(128)} %convert_maximum_fusion.1) | copy-start | bytes 1540
  298.3 13.6 %copy-start.17 = (s32[1024]{0:T(1024)S(1)}, s32[1024]{0:T(1024)}, u32[]{:S(2)}) copy-start(s32[1024]{0:T(1024)} %get-tuple-element.135) | copy-start | bytes 12292
  308.5 5.4 %copy-start.16 = (s32[1024]{0:T(1024)S(1)}, s32[1024]{0:T(1024)}, u32[]{:S(2)}) copy-start(s32[1024]{0:T(1024)} %get-tuple-element.134) | copy-start | bytes 12292
  315.9 7.8 %copy-start.23 = (f32[1,256]{1,0:T(1,128)S(1)}, f32[1,256]{1,0:T(1,128)}, u32[]{:S(2)}) copy-start(f32[1,256]{1,0:T(1,128)} %get-tuple-element.121) | copy-start | bytes 3076
  318.0 7.2 %copy-start.29 = (pred[256]{0:T(512)(128)(4,1)S(1)}, pred[256]{0:T(512)(128)(4,1)}, u32[]{:S(2)}) copy-start(pred[256]{0:T(512)(128)(4,1)} %compare_and_fusion.11) | copy-start | bytes 772
  (8 other events, 21.8 us)
Sparse Core Ops, SparseCore 0:
  237.7 26.8 reduce-scatter.1
